TPU v7x, 32 devices: a whole 2x2x4 slice. The times are simulated.
32 devices in a mesh: ga: 2 (over x), row: 8 (over z, y), col: 2 (over core).
Axes of the slice: x: 2, y: 2, z: 4, core: 2. Of those that a mesh axis runs over, the one named last changes fastest.
Arguments:
- pair: bfloat16 [256, 128, 128], P(('ga', 'row', 'col')), parts along dimension 0, may hold values from -480 to 480
- residue_mask: int32 [256], P('ga'), parts along dimension 0, may hold values from 0 to 1, as said below
- targets: int32 [256, 128], P(('ga', 'row', 'col')), parts along dimension 0, may hold values from 0 to 63
- ln_gain: float32 [2, 128], replicated, may hold values from 0.25 to 1.75
- ln_shift: float32 [2, 128], replicated, may hold values from -3 to 3
- w_in: bfloat16 [5, 128, 128], P(None, None, 'col'), may hold values from -0.5 to 0.5
- b_in: float32 [5, 128], replicated, may hold values from -3 to 3
- w_out: bfloat16 [128, 128], P('col'), may hold values from -0.5 to 0.5
- b_out: float32 [128], replicated, may hold values from -3 to 3
- head_weight: bfloat16 [128, 64], replicated, may hold values from -0.5 to 0.5
- head_bias: float32 [64], replicated, may hold values from -4 to 4
Outputs:
- update: bfloat16 [256, 128, 128], P(('ga', 'row', 'col')), parts along dimension 0
- pair_loss: float32 [256, 128], P(('ga', 'row', 'col')), parts along dimension 0
There are 2 independent parts, one for each index of `ga`. A program takes and returns all parts, laid end to end along the dimension named above; an argument that names none is the same for every part. Nothing has to cross between parts.
Inputs may be any that keep to these rules, and one draw needn't show every extreme that they name: `residue_mask`: each part's entries are 1 for residues 0 to some length - 1 and 0 after it; the length is at least 64 and at most 128.
All inputs are finite; a program needn't handle non-finite values.
Results may differ from a plain program's by a relative error of at most 0.0055.
Values may be sent and summed in bfloat16 or wider, within the bound.
A program may use at most 64 MiB of HBM per device.

v0:
```python
import jax
import jax.numpy as jnp
from jax import lax
from jax.sharding import PartitionSpec as P


def normalize(values, gain_vec, shift_vec, epsilon, reduce_axis):
    average = jnp.mean(values, axis=reduce_axis, keepdims=True)
    centred = values - average
    spread = jnp.mean(centred * centred, axis=reduce_axis, keepdims=True)
    return centred * lax.rsqrt(spread + epsilon) * gain_vec + shift_vec


def local(
    pair, residue_mask, targets, ln_gain, ln_shift, w_in, b_in, w_out, b_out, head_weight, head_bias
):
    row_count, length, pair_width = pair.shape
    groups = lax.axis_size(("row", "col"))
    chan_share = pair_width // groups
    res_mask = residue_mask.astype(jnp.float32)
    own_mask = lax.dynamic_slice_in_dim(
        res_mask, lax.axis_index(("row", "col")) * row_count, row_count
    )
    pair_mask = own_mask[:, None] * res_mask[None, :]
    normed = normalize(pair.astype(jnp.float32), ln_gain[0], ln_shift[0], 0.1, -1).astype(
        jnp.bfloat16
    )
    projected = jnp.einsum(
        "ikc,ncd->ndik",
        normed,
        lax.all_gather(w_in, "col", axis=2, tiled=True),
        preferred_element_type=jnp.float32,
    )
    projected = projected + b_in[:, :, None, None]
    left_side = pair_mask * jax.nn.sigmoid(projected[1]) * projected[0]
    right_side = pair_mask * jax.nn.sigmoid(projected[3]) * projected[2]
    stacked = jnp.stack([left_side, right_side, projected[4]])
    left_side = stacked[0].astype(jnp.bfloat16)
    right_side = stacked[1].astype(jnp.bfloat16)
    gate_pre = stacked[2]
    left_blocks = left_side.reshape(groups, chan_share, row_count, length)
    right_blocks = right_side.reshape(groups, chan_share, row_count, length)
    left_part = lax.all_to_all(left_blocks, ("row", "col"), split_axis=0, concat_axis=2, tiled=True)
    right_part = lax.all_to_all(
        right_blocks, ("row", "col"), split_axis=0, concat_axis=2, tiled=True
    )
    product = jnp.einsum(
        "xcik,xcjk->xcij", left_part, right_part, preferred_element_type=jnp.float32
    )
    returned = lax.all_to_all(
        product.astype(jnp.bfloat16), ("row", "col"), split_axis=2, concat_axis=0, tiled=True
    )
    outer_prod = returned.reshape(pair_width, row_count, length)
    normed_outer = normalize(
        outer_prod.astype(jnp.float32),
        ln_gain[1][:, None, None],
        ln_shift[1][:, None, None],
        1.0,
        0,
    ).astype(jnp.bfloat16)
    mixed = jnp.einsum(
        "cij,cd->dij",
        normed_outer,
        lax.all_gather(w_out, "col", axis=0, tiled=True),
        preferred_element_type=jnp.float32,
    )
    update_chan = jax.nn.sigmoid(gate_pre) * (mixed + b_out[:, None, None])
    update = jnp.transpose(update_chan, (1, 2, 0)).astype(jnp.bfloat16)
    new_pair = (pair.astype(jnp.float32) + update.astype(jnp.float32)).astype(jnp.bfloat16)
    logits = (
        jnp.einsum("ijc,cb->ijb", new_pair, head_weight, preferred_element_type=jnp.float32)
        + head_bias
    )
    mirrored = lax.all_to_all(
        logits.astype(jnp.bfloat16), ("row", "col"), split_axis=1, concat_axis=0, tiled=True
    ).astype(logits.dtype)
    symmetric = logits + jnp.transpose(mirrored, (1, 0, 2))
    row_top = jnp.max(symmetric, axis=-1, keepdims=True)
    log_total = row_top[..., 0] + jnp.log(jnp.sum(jnp.exp(symmetric - row_top), axis=-1))
    bin_index = jnp.arange(symmetric.shape[2], dtype=jnp.int32)
    picked = jnp.sum(jnp.where(targets[..., None] == bin_index, symmetric, 0.0), axis=-1)
    pair_loss = pair_mask * (log_total - picked)
    return (update, pair_loss)


def solution(mesh):
    placed = (
        P(("ga", "row", "col"), None, None),
        P("ga"),
        P(("ga", "row", "col"), None),
        P(),
        P(),
        P(None, None, "col"),
        P(),
        P("col", None),
        P(),
        P(),
        P(),
    )
    return jax.shard_map(
        local,
        mesh=mesh,
        in_specs=placed,
        out_specs=(P(("ga", "row", "col"), None, None), P(("ga", "row", "col"), None)),
        check_vma=False,
    )
```

profile of v0, /device:TPU:0, one launch (start us, length us, event | category | flops | bytes accessed | tf_op | source)
XLA Modules:
  0.0 68.8 jit_solution(7911302540243961104)
XLA Ops:
  0.6 1.1 %copy.51 = bf16[8,128,128]{1,2,0:T(8,128)(2,1)S(1)} copy(bf16[8,128,128]{2,1,0:T(8,128)(2,1)} %param.11) | data formatting | bytes 524288 | tf_op args[0]
  1.9 2.3 %all_gather.6 = bf16[5,128,128]{1,2,0:T(8,128)(2,1)S(1)} all-gather(bf16[5,128,64]{1,2,0:T(8,128)(2,1)} %param.16), channel_id=1, replica_groups=mesh['ga'=2,'row'=8,'col'=2] {'col'}, dimensions={2}, use_global_device_ids=true | all-gather | bytes 245760 | tf_op jit(solution)/shard_map/all_gather | solution.py:31
  4.2 0.8 %slice_bitcast_fusion.2 = (f32[128]{0:T(128)S(1)}, f32[128]{0:T(128)S(1)}, f32[128]{0:T(128)S(1)}, f32[128]{0:T(128)S(1)}) fusion(f32[2,128]{1,0:T(2,128)} %param.15, f32[2,128]{1,0:T(2,128)} %param.14), kind=kLoop, calls=%fused_computation.74 | loop fusion | bytes 4096 | tf_op jit(solution)/shard_map/add | solution.py:11
  5.0 1.3 %add_bitcast_fusion = f32[5,128,8,128]{3,1,0,2:T(8,128)S(1)} fusion(f32[5,128]{1,0:T(8,128)} %param.17, bf16[8,128,128]{1,2,0:T(8,128)(2,1)S(1)} %copy.51, f32[128]{0:T(128)S(1)} %get-tuple-element.21, f32[128]{0:T(128)S(1)} %get-tuple-element.24, f32[8,128]{1,0:T(8,128)S(1)} %add_rsqrt_fusion.1, f32[8,128]{1,0:T(8,128)S(1)} %broadcast_multiply_fusion.2, ...), kind=kOutput, calls=%fused_computation | convolution fusion | flops 169213952 | bytes 3059200 | tf_op jit(solution)/shard_map/ikc,ncd->ndik/dot_general | solution.py:28
  6.3 1.3 %fusion.19 = (f32[16,8,8,128]{3,1,0,2:T(8,128)S(1)}, f32[16,8,8,128]{3,1,0,2:T(8,128)}, f32[16,8,8,128]{3,1,0,2:T(8,128)}, f32[16,8,8,128]{3,1,0,2:T(8,128)}) fusion(f32[5,128,8,128]{3,1,0,2:T(8,128)S(1)} %add_bitcast_fusion), kind=kLoop, calls=%fused_computation.30 | loop fusion | flops 786432 | bytes 4194304 | tf_op jit(solution)/shard_map/div | solution.py:35
  7.7 1.5 %fusion.29 = (bf16[16,8,8,128]{3,1,2,0:T(8,128)(2,1)S(1)}, bf16[16,8,8,128]{3,1,2,0:T(8,128)(2,1)S(1)}) fusion(f32[16,8,8,128]{3,1,0,2:T(8,128)} %get-tuple-element.15, f32[16,8,8,128]{3,1,0,2:T(8,128)S(1)} %get-tuple-element.12, f32[8,128]{1,0:T(8,128)S(1)} %broadcast_multiply_fusion, f32[16,8,8,128]{3,1,0,2:T(8,128)} %get-tuple-element.13, ...), kind=kLoop, calls=%fused_computation.47 | loop fusion | flops 786432 | bytes 2625536 | tf_op jit(solution)/shard_map/convert_element_type | solution.py:38
  9.2 17.1 %all_to_all.48 = bf16[16,8,8,128]{3,1,2,0:T(8,128)(2,1)S(1)} all-to-all(bf16[16,8,8,128]{3,1,2,0:T(8,128)(2,1)S(1)} %get-tuple-element.17), channel_id=1, replica_groups=mesh['ga'=2,'row'=8,'col'=2] {'row','col'}, dimensions={0} | all-to-all | bytes 524288 | tf_op jit(solution)/shard_map/all_to_all | solution.py:44
  26.3 12.7 %all_to_all.49 = bf16[16,8,8,128]{3,1,2,0:T(8,128)(2,1)S(1)} all-to-all(bf16[16,8,8,128]{3,1,2,0:T(8,128)(2,1)S(1)} %get-tuple-element.16), channel_id=1, replica_groups=mesh['ga'=2,'row'=8,'col'=2] {'row','col'}, dimensions={0} | all-to-all | bytes 524288 | tf_op jit(solution)/shard_map/all_to_all | solution.py:43
  39.0 0.3 fusion.3
  39.3 0.9 %copy.59 = bf16[1,8,128,128]{3,1,0,2:T(8,128)(2,1)} copy(bf16[1,8,128,128]{3,2,1,0:T(8,128)(2,1)S(1)} %fusion.3) | data formatting | bytes 524288 | tf_op jit(solution)/shard_map/convert_element_type | solution.py:51
  40.2 3.5 %all-to-all-start.2 = ((bf16[1,8,128,128]{3,1,0,2:T(8,128)(2,1)}), bf16[1,8,128,128]{3,1,0,2:T(8,128)(2,1)S(1)}, u32[]{:S(2)}, u32[]{:S(2)}) async-start(bf16[1,8,128,128]{3,1,0,2:T(8,128)(2,1)} %copy.59), calls=%async_computation.2 | async-start | bytes 524288 | tf_op jit(solution)/shard_map/all_to_all | solution.py:50
  43.8 1.8 %all_gather.7 = bf16[128,128]{1,0:T(8,128)(2,1)S(1)} all-gather(bf16[64,128]{1,0:T(8,128)(2,1)S(1)} %copy-done.1), channel_id=1, replica_groups=mesh['ga'=2,'row'=8,'col'=2] {'col'}, dimensions={0}, use_global_device_ids=true | all-gather | bytes 49152 | tf_op jit(solution)/shard_map/all_gather | solution.py:64
  45.6 8.1 %all-to-all-done.2 = bf16[1,8,128,128]{3,1,0,2:T(8,128)(2,1)S(1)} async-done(((bf16[1,8,128,128]{3,1,0,2:T(8,128)(2,1)}), bf16[1,8,128,128]{3,1,0,2:T(8,128)(2,1)S(1)}, u32[]{:S(2)}, u32[]{:S(2)}) %all-to-all-start.2) | async-done | bytes 262176 | tf_op jit(solution)/shard_map/all_to_all | solution.py:50
  54.1 0.3 fusion.27
  54.5 0.3 fusion.4
  54.8 0.2 fusion.47
  55.0 0.2 copy.65
  55.2 0.9 %reshape.121 = bf16[16,2,2048]{2,1,0:T(2,128)(2,1)} reshape(bf16[128,8,64]{2,1,0:T(8,128)(2,1)S(1)} %bitcast.103) | data formatting | bytes 262144
  56.1 3.5 %all-to-all-start.3 = ((bf16[16,2,2048]{2,1,0:T(2,128)(2,1)}), bf16[16,2,2048]{2,1,0:T(2,128)(2,1)S(1)}, u32[]{:S(2)}, u32[]{:S(2)}) async-start(bf16[16,2,2048]{2,1,0:T(2,128)(2,1)} %reshape.121), calls=%async_computation.3 | async-start | bytes 262144 | tf_op jit(solution)/shard_map/all_to_all | solution.py:74
  59.6 0.9 %copy.69 = bf16[8,128,128]{2,1,0:T(8,128)(2,1)} copy(bf16[8,128,128]{1,2,0:T(8,128)(2,1)S(1)} %fusion.4) | data formatting | bytes 524288
  60.5 7.0 %all-to-all-done.3 = bf16[16,2,2048]{2,1,0:T(2,128)(2,1)S(1)} async-done(((bf16[16,2,2048]{2,1,0:T(2,128)(2,1)}), bf16[16,2,2048]{2,1,0:T(2,128)(2,1)S(1)}, u32[]{:S(2)}, u32[]{:S(2)}) %all-to-all-start.3) | async-done | bytes 131104 | tf_op jit(solution)/shard_map/all_to_all | solution.py:74
  67.5 0.2 reshape.122
  67.8 0.2 copy.68
  68.2 0.7 subtract_multiply_fusion
  (29 shorter events, 0.9 us)
Async XLA Ops:
  0.6 54.2 %copy-start = (bf16[128,64]{0,1:T(8,128)(2,1)S(1)}, bf16[128,64]{0,1:T(8,128)(2,1)}, u32[]{:S(2)}) copy-start(bf16[128,64]{0,1:T(8,128)(2,1)} %param.20) | copy-start | bytes 49156
  6.2 1.3 %copy-start.4 = (s32[128]{0:T(128)S(1)}, s32[128]{0:T(128)}, u32[]{:S(2)}) copy-start(s32[128]{0:T(128)} %param.12) | copy-start | bytes 1540
  7.7 36.0 %copy-start.1 = (bf16[64,128]{1,0:T(8,128)(2,1)S(1)}, bf16[64,128]{1,0:T(8,128)(2,1)}, u32[]{:S(2)}) copy-start(bf16[64,128]{1,0:T(8,128)(2,1)} %param.18) | copy-start | bytes 49156
  39.0 15.4 %copy-start.5 = (f32[128]{0:T(128)S(1)}, f32[128]{0:T(128)}, u32[]{:S(2)}) copy-start(f32[128]{0:T(128)} %param.19) | copy-start | bytes 1540
  40.2 13.5 %all-to-all-start.2 = ((bf16[1,8,128,128]{3,1,0,2:T(8,128)(2,1)}), bf16[1,8,128,128]{3,1,0,2:T(8,128)(2,1)S(1)}, u32[]{:S(2)}, u32[]{:S(2)}) async-start(bf16[1,8,128,128]{3,1,0,2:T(8,128)(2,1)} %copy.59), calls=%async_computation.2 | async-start | bytes 524288 | tf_op jit(solution)/shard_map/all_to_all | solution.py:50
  54.0 0.8 %copy-start.3 = (f32[64]{0:T(128)S(1)}, f32[64]{0:T(128)}, u32[]{:S(2)}) copy-start(f32[64]{0:T(128)} %param.21) | copy-start | bytes 772
  55.0 13.1 %copy-start.2 = (s32[8,128]{1,0:T(8,128)S(1)}, s32[8,128]{1,0:T(8,128)}, u32[]{:S(2)}) copy-start(s32[8,128]{1,0:T(8,128)} %param.13) | copy-start | bytes 12292
  56.1 11.4 %all-to-all-start.3 = ((bf16[16,2,2048]{2,1,0:T(2,128)(2,1)}), bf16[16,2,2048]{2,1,0:T(2,128)(2,1)S(1)}, u32[]{:S(2)}, u32[]{:S(2)}) async-start(bf16[16,2,2048]{2,1,0:T(2,128)(2,1)} %reshape.121), calls=%async_computation.3 | async-start | bytes 262144 | tf_op jit(solution)/shard_map/all_to_all | solution.py:74
where the time goes:
time: 69.3 us; the launch traced here: 68.8 us
  blocking collectives  33.9 us (49%)
  waiting for transfers between devices  15.2 us (22%)
  starting transfers between devices  7.04 us (10%)
  local copies, waits for them, and re-layouts  5.29 us (8%)
  other arithmetic  4.54 us (7%)
  matrix products  2.07 us (3%)
  between operations  0.87 us (1%)
    all_to_all x1, blocking collectives, local(): lax.all_to_all(right_blocks, ('row', 'col'), split_axis=0, concat_axis=2,...  17.1 us
    all_to_all x1, blocking collectives, local(): lax.all_to_all(left_blocks, ('row', 'col'), split_axis=0, concat_axis=2,...  12.7 us
    all_to_all x1, waiting for transfers between devices, local(): lax.all_to_all(product.astype(jnp.bfloat16), ('row', 'col'), split_axis=2...  8.14 us
    all_to_all x1, waiting for transfers between devices, local(): lax.all_to_all(logits.astype(jnp.bfloat16), ('row', 'col'), split_axis=1,...  7.02 us
    all_to_all x1, starting transfers between devices, local(): lax.all_to_all(product.astype(jnp.bfloat16), ('row', 'col'), split_axis=2...  3.53 us
    all_to_all x1, starting transfers between devices, local(): lax.all_to_all(logits.astype(jnp.bfloat16), ('row', 'col'), split_axis=1,...  3.51 us
    unnamed x16, local copies, waits for them, and re-layouts  3.09 us
    all_gather x1, blocking collectives, local(): lax.all_gather(w_in, 'col', axis=2, tiled=True)  2.27 us
  transfers between devices with their start and end apart: 2, of which 2 were waited for; matrix products, arithmetic and copies ran while one was open for 1% of the time, Pallas kernels for 0%

commit v1 on v0

--- a/solution.py
+++ b/solution.py
@@ -71,8 +71,16 @@
         jnp.einsum("ijc,cb->ijb", new_pair, head_weight, preferred_element_type=jnp.float32)
         + head_bias
     )
-    mirrored = lax.all_to_all(
-        logits.astype(jnp.bfloat16), ("row", "col"), split_axis=1, concat_axis=0, tiled=True
+    mirrored = jnp.concatenate(
+        lax.all_to_all(
+            jnp.stack(
+                jnp.split(logits.astype(jnp.bfloat16), lax.axis_size(("row", "col")), axis=1)
+            ),
+            ("row", "col"),
+            0,
+            0,
+        ),
+        axis=0,
     ).astype(logits.dtype)
     symmetric = logits + jnp.transpose(mirrored, (1, 0, 2))
     row_top = jnp.max(symmetric, axis=-1, keepdims=True)

time: 69.3 us -> 71.6 us (1.033)
  local copies, waits for them, and re-layouts: 5.29 us -> 7.45 us
    another operation x0 -> x18, local copies, waits for them, and re-layouts: none -> 2.27 us  [local(): jnp.stack(jnp.split(logits.astype(jnp.bfloat16), lax.axis_size(('row', 'c...]
    unnamed x16 -> x31, local copies, waits for them, and re-layouts: 3.09 us -> 3.23 us
where the time goes in v1:
time: 71.6 us; the launch traced here: 71.1 us
  blocking collectives  33.9 us (47%)
  waiting for transfers between devices  15.2 us (21%)
  local copies, waits for them, and re-layouts  7.45 us (10%)
  starting transfers between devices  7.04 us (10%)
  other arithmetic  4.57 us (6%)
  matrix products  2.07 us (3%)
  between operations  0.94 us (1%)
    all_to_all x1, blocking collectives, local(): lax.all_to_all(right_blocks, ('row', 'col'), split_axis=0, concat_axis=2,...  17.1 us
    all_to_all x1, blocking collectives, local(): lax.all_to_all(left_blocks, ('row', 'col'), split_axis=0, concat_axis=2,...  12.7 us
    all_to_all x1, waiting for transfers between devices, local(): lax.all_to_all(product.astype(jnp.bfloat16), ('row', 'col'), split_axis=2...  8.14 us
    all_to_all x1, waiting for transfers between devices, local(): lax.all_to_all(jnp.stack(jnp.split(logits.astype(jnp.bfloat16), lax.axis_...  7.02 us
    all_to_all x1, starting transfers between devices, local(): lax.all_to_all(product.astype(jnp.bfloat16), ('row', 'col'), split_axis=2...  3.53 us
    all_to_all x1, starting transfers between devices, local(): lax.all_to_all(jnp.stack(jnp.split(logits.astype(jnp.bfloat16), lax.axis_...  3.51 us
    unnamed x31, local copies, waits for them, and re-layouts  3.23 us
    all_gather x1, blocking collectives, local(): lax.all_gather(w_in, 'col', axis=2, tiled=True)  2.27 us
  transfers between devices with their start and end apart: 2, of which 2 were waited for; matrix products, arithmetic and copies ran while one was open for 1% of the time, Pallas kernels for 0%

profile of v1, /device:TPU:0, one launch (start us, length us, event | category | flops | bytes accessed | tf_op | source)
XLA Modules:
  0.0 71.1 jit_solution(11830761542855965868)
XLA Ops:
  0.6 1.1 %copy.63 = bf16[8,128,128]{1,2,0:T(8,128)(2,1)S(1)} copy(bf16[8,128,128]{2,1,0:T(8,128)(2,1)} %param.11) | data formatting | bytes 524288 | tf_op args[0]
  1.9 2.3 %all_gather.6 = bf16[5,128,128]{1,2,0:T(8,128)(2,1)S(1)} all-gather(bf16[5,128,64]{1,2,0:T(8,128)(2,1)} %param.16), channel_id=1, replica_groups=mesh['ga'=2,'row'=8,'col'=2] {'col'}, dimensions={2}, use_global_device_ids=true | all-gather | bytes 245760 | tf_op jit(solution)/shard_map/all_gather | solution.py:31
  4.2 0.8 %slice_bitcast_fusion.18 = (f32[128]{0:T(128)S(1)}, f32[128]{0:T(128)S(1)}, f32[128]{0:T(128)S(1)}, f32[128]{0:T(128)S(1)}) fusion(f32[2,128]{1,0:T(2,128)} %param.15, f32[2,128]{1,0:T(2,128)} %param.14), kind=kLoop, calls=%fused_computation.106 | loop fusion | bytes 4096 | tf_op jit(solution)/shard_map/add | solution.py:11
  5.0 1.3 %add_bitcast_fusion = f32[5,128,8,128]{3,1,0,2:T(8,128)S(1)} fusion(f32[5,128]{1,0:T(8,128)} %param.17, bf16[8,128,128]{1,2,0:T(8,128)(2,1)S(1)} %copy.63, f32[128]{0:T(128)S(1)} %get-tuple-element.37, f32[128]{0:T(128)S(1)} %get-tuple-element.40, f32[8,128]{1,0:T(8,128)S(1)} %add_rsqrt_fusion.1, f32[8,128]{1,0:T(8,128)S(1)} %broadcast_multiply_fusion.2, ...), kind=kOutput, calls=%fused_computation | convolution fusion | flops 169213952 | bytes 3059200 | tf_op jit(solution)/shard_map/ikc,ncd->ndik/dot_general | solution.py:28
  6.3 1.3 %fusion.19 = (f32[16,8,8,128]{3,1,0,2:T(8,128)S(1)}, f32[16,8,8,128]{3,1,0,2:T(8,128)}, f32[16,8,8,128]{3,1,0,2:T(8,128)}, f32[16,8,8,128]{3,1,0,2:T(8,128)}) fusion(f32[5,128,8,128]{3,1,0,2:T(8,128)S(1)} %add_bitcast_fusion), kind=kLoop, calls=%fused_computation.30 | loop fusion | flops 786432 | bytes 4194304 | tf_op jit(solution)/shard_map/div | solution.py:35
  7.7 1.5 %fusion.29 = (bf16[16,8,8,128]{3,1,2,0:T(8,128)(2,1)S(1)}, bf16[16,8,8,128]{3,1,2,0:T(8,128)(2,1)S(1)}) fusion(f32[16,8,8,128]{3,1,0,2:T(8,128)} %get-tuple-element.15, f32[16,8,8,128]{3,1,0,2:T(8,128)S(1)} %get-tuple-element.12, f32[8,128]{1,0:T(8,128)S(1)} %broadcast_multiply_fusion, f32[16,8,8,128]{3,1,0,2:T(8,128)} %get-tuple-element.13, ...), kind=kLoop, calls=%fused_computation.46 | loop fusion | flops 786432 | bytes 2625536 | tf_op jit(solution)/shard_map/convert_element_type | solution.py:38
  9.3 17.1 %all_to_all.44 = bf16[16,8,8,128]{3,1,2,0:T(8,128)(2,1)S(1)} all-to-all(bf16[16,8,8,128]{3,1,2,0:T(8,128)(2,1)S(1)} %get-tuple-element.33), channel_id=1, replica_groups=mesh['ga'=2,'row'=8,'col'=2] {'row','col'}, dimensions={0} | all-to-all | bytes 524288 | tf_op jit(solution)/shard_map/all_to_all | solution.py:44
  26.4 12.7 %all_to_all.45 = bf16[16,8,8,128]{3,1,2,0:T(8,128)(2,1)S(1)} all-to-all(bf16[16,8,8,128]{3,1,2,0:T(8,128)(2,1)S(1)} %get-tuple-element.32), channel_id=1, replica_groups=mesh['ga'=2,'row'=8,'col'=2] {'row','col'}, dimensions={0} | all-to-all | bytes 524288 | tf_op jit(solution)/shard_map/all_to_all | solution.py:43
  39.0 0.3 fusion.3
  39.3 0.9 %copy.71 = bf16[1,8,128,128]{3,1,0,2:T(8,128)(2,1)} copy(bf16[1,8,128,128]{3,2,1,0:T(8,128)(2,1)S(1)} %fusion.3) | data formatting | bytes 524288 | tf_op jit(solution)/shard_map/convert_element_type | solution.py:51
  40.2 3.5 %all-to-all-start.2 = ((bf16[1,8,128,128]{3,1,0,2:T(8,128)(2,1)}), bf16[1,8,128,128]{3,1,0,2:T(8,128)(2,1)S(1)}, u32[]{:S(2)}, u32[]{:S(2)}) async-start(bf16[1,8,128,128]{3,1,0,2:T(8,128)(2,1)} %copy.71), calls=%async_computation.2 | async-start | bytes 524288 | tf_op jit(solution)/shard_map/all_to_all | solution.py:50
  43.8 1.8 %all_gather.7 = bf16[128,128]{1,0:T(8,128)(2,1)S(1)} all-gather(bf16[64,128]{1,0:T(8,128)(2,1)S(1)} %copy-done.1), channel_id=1, replica_groups=mesh['ga'=2,'row'=8,'col'=2] {'col'}, dimensions={0}, use_global_device_ids=true | all-gather | bytes 49152 | tf_op jit(solution)/shard_map/all_gather | solution.py:64
  45.6 8.1 %all-to-all-done.2 = bf16[1,8,128,128]{3,1,0,2:T(8,128)(2,1)S(1)} async-done(((bf16[1,8,128,128]{3,1,0,2:T(8,128)(2,1)}), bf16[1,8,128,128]{3,1,0,2:T(8,128)(2,1)S(1)}, u32[]{:S(2)}, u32[]{:S(2)}) %all-to-all-start.2) | async-done | bytes 262176 | tf_op jit(solution)/shard_map/all_to_all | solution.py:50
  54.1 0.3 fusion.27
  54.5 0.3 fusion.4
  54.8 0.2 fusion.47
  55.0 0.6 slice_bitcast_fusion.2
  57.5 0.9 %reshape.119 = bf16[16,2,2048]{2,1,0:T(2,128)(2,1)} reshape(bf16[16,8,8,64]{3,2,1,0:T(8,128)(2,1)S(1)} %constant_dynamic-update-slice_fusion) | data formatting | bytes 262144
  58.4 3.5 %all-to-all-start.3 = ((bf16[16,2,2048]{2,1,0:T(2,128)(2,1)}), bf16[16,2,2048]{2,1,0:T(2,128)(2,1)S(1)}, u32[]{:S(2)}, u32[]{:S(2)}) async-start(bf16[16,2,2048]{2,1,0:T(2,128)(2,1)} %reshape.119), calls=%async_computation.3 | async-start | bytes 262144 | tf_op jit(solution)/shard_map/all_to_all | solution.py:75
  61.9 0.8 %copy.94 = bf16[8,128,128]{2,1,0:T(8,128)(2,1)} copy(bf16[8,128,128]{1,2,0:T(8,128)(2,1)S(1)} %fusion.4) | data formatting | bytes 524288
  62.8 7.0 %all-to-all-done.3 = bf16[16,2,2048]{2,1,0:T(2,128)(2,1)S(1)} async-done(((bf16[16,2,2048]{2,1,0:T(2,128)(2,1)}), bf16[16,2,2048]{2,1,0:T(2,128)(2,1)S(1)}, u32[]{:S(2)}, u32[]{:S(2)}) %all-to-all-start.3) | async-done | bytes 131104 | tf_op jit(solution)/shard_map/all_to_all | solution.py:75
  69.8 0.2 reshape.120
  70.1 0.2 copy.93
  70.4 0.7 subtract_multiply_fusion
  (60 shorter events, 2.7 us)
Async XLA Ops:
  0.6 54.2 %copy-start = (bf16[128,64]{0,1:T(8,128)(2,1)S(1)}, bf16[128,64]{0,1:T(8,128)(2,1)}, u32[]{:S(2)}) copy-start(bf16[128,64]{0,1:T(8,128)(2,1)} %param.20) | copy-start | bytes 49156
  6.2 1.3 %copy-start.4 = (s32[128]{0:T(128)S(1)}, s32[128]{0:T(128)}, u32[]{:S(2)}) copy-start(s32[128]{0:T(128)} %param.12) | copy-start | bytes 1540
  7.7 36.0 %copy-start.1 = (bf16[64,128]{1,0:T(8,128)(2,1)S(1)}, bf16[64,128]{1,0:T(8,128)(2,1)}, u32[]{:S(2)}) copy-start(bf16[64,128]{1,0:T(8,128)(2,1)} %param.18) | copy-start | bytes 49156
  39.0 15.4 %copy-start.5 = (f32[128]{0:T(128)S(1)}, f32[128]{0:T(128)}, u32[]{:S(2)}) copy-start(f32[128]{0:T(128)} %param.19) | copy-start | bytes 1540
  40.2 13.5 %all-to-all-start.2 = ((bf16[1,8,128,128]{3,1,0,2:T(8,128)(2,1)}), bf16[1,8,128,128]{3,1,0,2:T(8,128)(2,1)S(1)}, u32[]{:S(2)}, u32[]{:S(2)}) async-start(bf16[1,8,128,128]{3,1,0,2:T(8,128)(2,1)} %copy.71), calls=%async_computation.2 | async-start | bytes 524288 | tf_op jit(solution)/shard_map/all_to_all | solution.py:50
  54.0 0.8 %copy-start.3 = (f32[64]{0:T(128)S(1)}, f32[64]{0:T(128)}, u32[]{:S(2)}) copy-start(f32[64]{0:T(128)} %param.21) | copy-start | bytes 772
  56.6 13.8 %copy-start.2 = (s32[8,128]{1,0:T(8,128)S(1)}, s32[8,128]{1,0:T(8,128)}, u32[]{:S(2)}) copy-start(s32[8,128]{1,0:T(8,128)} %param.13) | copy-start | bytes 12292
  58.4 11.4 %all-to-all-start.3 = ((bf16[16,2,2048]{2,1,0:T(2,128)(2,1)}), bf16[16,2,2048]{2,1,0:T(2,128)(2,1)S(1)}, u32[]{:S(2)}, u32[]{:S(2)}) async-start(bf16[16,2,2048]{2,1,0:T(2,128)(2,1)} %reshape.119), calls=%async_computation.3 | async-start | bytes 262144 | tf_op jit(solution)/shard_map/all_to_all | solution.py:75
